TPU v7x, 256 devices: a whole 4x4x8 slice. The times are simulated.
256 devices in a mesh: span: 8 (over y, core), chord: 32 (over z, x).
Axes of the slice: x: 4, y: 4, z: 8, core: 2. Of those that a mesh axis runs over, the one named last changes fastest.
Arguments:
- node_pos: float32 [3, 524288], P(None, ('span', 'chord')), may hold values from -0.4 to 0.4
- ctrl_pos: float32 [3, 8192], P(None, ('span', 'chord')), may hold values from -0.4 to 0.4
- ctrl_ids: int32 [8192], P(('span', 'chord')), may hold values from 0 to 1023
- wing_shift: float32 [15, 1024], replicated, may hold values from -0.06 to 0.06
- wing_speed: float32 [15, 1024], replicated, may hold values from -0.6 to 0.6
- minv: float32 [8192, 8192], P(('span', 'chord')), may hold values from -1 to 3, as said below
- conn: int32 [64, 32768], P(None, ('span', 'chord')), may hold values from 0 to 2047
- face_elem: int32 [8, 32, 4, 32], P('span', 'chord'), may hold values from 0 to 127
- face_match: int32 [8, 32, 4, 32], P('span', 'chord'), may hold values from 0 to 31, each once within a row
Outputs:
- det_jac: float32 [5, 64, 32768], P(None, None, ('span', 'chord'))
- grid_flux: float32 [5, 3, 64, 32768], P(None, None, None, ('span', 'chord'))
- face_flux: float32 [8, 32, 4, 5, 16, 32], P('span', 'chord')
Inputs may be any that keep to these rules, and one draw needn't show every extreme that they name: minv is exactly symmetric. Each face_match[j, k, t, :] is a permutation of 0 to 31.
All inputs are finite; a program needn't handle non-finite values.
Results may differ from a plain program's by a relative error of at most 0.00025.
Values sent between devices are 32-bit elements; how exact they have to be, the bound alone decides.
A program may use at most 64 MiB of HBM per device.

v0:
```python
import math
import jax
import jax.numpy as jnp
import numpy as np
from jax import lax
from jax.sharding import Mesh
from jax.sharding import PartitionSpec as P

SPAN_CHORD = ("span_0", "span_1", "chord_0", "chord_1")
SPAN = ("span_0", "span_1")
CHORD = ("chord_0", "chord_1")
kernel_width = 0.1


def in_order(parts, dim):
    shape = list(parts.shape[1:])
    shape[dim] *= parts.shape[0]
    return jnp.moveaxis(parts, 0, dim).reshape(shape)


def stacked_from(shard, axes, sequence):
    parts = shard
    for k in sequence:
        parts = lax.all_gather(parts, axes[k])
    done = sequence[::-1]
    back = [done.index(k) for k in range(len(axes))]
    parts = parts.transpose(*back, *range(len(axes), parts.ndim))
    return parts.reshape(-1, *shard.shape)


def gather_axes(shard, axes, sequence, dim):
    return in_order(stacked_from(shard, axes, sequence), dim)


def gather_turned(arrays, axis, dims):
    turned = [jnp.moveaxis(a, dim, 0) for a, dim in zip(arrays, dims)]
    widths = [t[0].size for t in turned]
    both = jnp.concatenate([t.reshape(-1, w) for t, w in zip(turned, widths)], axis=1)
    whole = lax.all_gather(both, axis, axis=0, tiled=True)
    parts = jnp.split(whole, [sum(widths[:k]) for k in range(1, len(widths))], axis=1)
    return tuple(
        (
            jnp.moveaxis(b.reshape(-1, *t.shape[1:]), 0, dim)
            for b, t, dim in zip(parts, turned, dims)
        )
    )


def passed_along(block, axis, distance):
    devices = range(lax.axis_size(axis))
    route = [(i - distance, i) for i in devices if i - distance in devices]
    return lax.ppermute(block, axis, route)


def passed_along_2(value, axis, steps):
    count = lax.axis_size(axis)
    pairs = [(source, (source + steps) % count) for source in range(count)]
    return lax.ppermute(value, axis, pairs)


def lobatto_table():
    points = np.array([-1.0, -1.0 / np.sqrt(5.0), 1.0 / np.sqrt(5.0), 1.0])
    barycentric = np.array(
        [
            1.0
            / np.prod([points[target] - points[source] for source in range(4) if source != target])
            for target in range(4)
        ]
    )
    derivative = np.zeros((4, 4))
    for target in range(4):
        for source in range(4):
            if source != target:
                derivative[target, source] = (
                    barycentric[source] / barycentric[target] / (points[target] - points[source])
                )
        derivative[target, target] = -np.sum(derivative[target])
    identity = np.eye(4)
    stacked = np.stack(
        [
            np.kron(np.kron(derivative, identity), identity),
            np.kron(np.kron(identity, derivative), identity),
            np.kron(np.kron(identity, identity), derivative),
        ]
    )
    return stacked.reshape(192, 64)


def element_metrics(node_rows, positions, links):
    sections = node_rows.shape[0] // 6
    elements = links.shape[1]
    moved = node_rows[: 3 * sections] + jnp.tile(positions, (sections, 1))
    gathered = jnp.take(jnp.concatenate([moved, node_rows[3 * sections :]], axis=0), links, axis=1)
    table = jnp.asarray(lobatto_table(), jnp.float32)
    jacobian = jnp.einsum(
        "rq,kqe->rke", table, gathered[: 3 * sections], precision=lax.Precision.HIGHEST
    )
    jacobian = jacobian.reshape(3, 64, sections, 3, elements).transpose(2, 3, 0, 1, 4)
    velocity = gathered[3 * sections :].reshape(sections, 3, 64, elements)

    def entry(spatial, along):
        return jacobian[:, spatial % 3, along % 3]

    metric = [
        [
            entry(spatial + 1, along + 1) * entry(spatial + 2, along + 2)
            - entry(spatial + 1, along + 2) * entry(spatial + 2, along + 1)
            for spatial in range(3)
        ]
        for along in range(3)
    ]
    volume = entry(0, 0) * metric[0][0] + entry(0, 1) * metric[1][0] + entry(0, 2) * metric[2][0]
    flux = jnp.stack(
        [
            metric[along][0] * velocity[:, 0]
            + metric[along][1] * velocity[:, 1]
            + metric[along][2] * velocity[:, 2]
            for along in range(3)
        ],
        axis=1,
    )
    return (volume, flux)


def face_traces(flux, sides):
    sections, elements = (flux.shape[0], flux.shape[3])
    cube = flux.reshape(sections, 3, 4, 4, 4, elements)
    surfaces = [-cube[:, 2, :, :, 0], cube[:, 2, :, :, 3], -cube[:, 1, :, 0], cube[:, 1, :, 3]]
    return jnp.stack(
        [
            jnp.take(surface.reshape(sections, 16, elements), sides[ordinal], axis=2)
            for ordinal, surface in enumerate(surfaces)
        ]
    )


def kernel_sum(weights_piece, points_piece, nodes):
    columns = points_piece.shape[1]
    block_width = math.gcd(columns, 256)

    def step(counter, total):
        offset = counter * block_width
        weight_block = lax.dynamic_slice_in_dim(weights_piece, offset, block_width, 1)
        point_block = lax.dynamic_slice_in_dim(points_piece, offset, block_width, 1)
        distance = (
            (point_block[0][:, None] - nodes[0][None, :]) ** 2
            + (point_block[1][:, None] - nodes[1][None, :]) ** 2
            + (point_block[2][:, None] - nodes[2][None, :]) ** 2
        )
        kernel = jnp.exp(-distance / (2.0 * kernel_width**2))
        return total + jnp.dot(
            weight_block,
            kernel,
            precision=lax.Precision.HIGHEST,
            preferred_element_type=jnp.float32,
        )

    empty = jnp.zeros((weights_piece.shape[0], nodes.shape[1]), jnp.float32)
    return lax.fori_loop(0, columns // block_width, step, empty)


def on_device(
    node_pos, ctrl_pos, ctrl_ids, wing_shift, wing_speed, minv, conn, face_elem, face_match
):
    highest = lax.Precision.HIGHEST
    table = jnp.concatenate([wing_shift, wing_speed], axis=0)
    every_id = gather_axes(ctrl_ids, SPAN_CHORD, (0, 2, 3, 1), 0)
    right_side = jnp.take(table, every_id, axis=1)
    own_weights = lax.dot_general(
        right_side,
        minv,
        (((1,), (1,)), ((), ())),
        precision=highest,
        preferred_element_type=jnp.float32,
    )
    pieces = gather_turned((own_weights, ctrl_pos), SPAN_CHORD, (1, 1))
    motion = kernel_sum(pieces[0], pieces[1], node_pos)
    volume, flux = element_metrics(motion, node_pos, conn)
    own = face_traces(flux, face_elem[0, 0])
    lower = passed_along(own[1], SPAN, 1)
    upper = passed_along(own[0], SPAN, -1)
    before = passed_along_2(own[3], CHORD, 1)
    after = passed_along_2(own[2], CHORD, -1)
    received = jnp.stack([lower, upper, before, after])
    matched = jnp.stack(
        [jnp.take(received[ordinal], face_match[0, 0, ordinal], axis=2) for ordinal in range(4)]
    )
    position = lax.axis_index(SPAN)
    span_count = lax.axis_size(SPAN)
    side_index = jnp.arange(4, dtype=jnp.int32)
    boundary = (side_index == 0) & (position == 0) | (side_index == 1) & (
        position == span_count - 1
    )
    opposite = jnp.where(boundary[:, None, None, None], -own, matched)
    face_flux = (0.5 * (own - opposite))[None, None]
    return (volume, flux, face_flux)


def solution(mesh):
    split = Mesh(mesh.devices.reshape(4, 2, 8, 4), ("span_0", "span_1", "chord_0", "chord_1"))
    return jax.shard_map(
        on_device,
        mesh=split,
        in_specs=(
            P(None, SPAN_CHORD),
            P(None, SPAN_CHORD),
            P(SPAN_CHORD),
            P(),
            P(),
            P(SPAN_CHORD, None),
            P(None, SPAN_CHORD),
            P(SPAN, CHORD, None, None),
            P(SPAN, CHORD, None, None),
        ),
        out_specs=(
            P(None, None, SPAN_CHORD),
            P(None, None, None, SPAN_CHORD),
            P(SPAN, CHORD, None, None, None, None),
        ),
        check_vma=False,
    )
```

profile of v0, /device:TPU:1, one launch (start us, length us, event | category | flops | bytes accessed | tf_op | source)
XLA Modules:
  0.0 360.8 jit_solution(5451668358771411971)
XLA Ops:
  10.1 7.8 %all-reduce = s32[128]{0:T(128)S(1)} all-reduce(s32[128]{0:T(128)S(1)} %dynamic-update-slice), channel_id=2, replica_groups=mesh['span_0'=4,'span_1'=2,'chord_0'=8,'chord_1'=4] {'span_0'}, use_global_device_ids=true, to_apply=%add | all-reduce | flops 128 | bytes 1024
  18.0 19.8 %all-gather.4 = s32[8,4,32]{2,1,0:T(4,128)S(1)} all-gather(s32[1,4,32]{2,1,0:T(4,128)S(1)} %reshape.722), channel_id=3, replica_groups=mesh['span_0'=4,'span_1'=2,'chord_0'=8,'chord_1'=4] {'chord_0'}, dimensions={0}, use_global_device_ids=true | all-gather | bytes 4608 | tf_op jit(solution)/shard_map/all_gather | solution.py:24
  37.8 9.3 %all-gather.2 = s32[32,4,32]{2,1,0:T(4,128)S(1)} all-gather(s32[8,4,32]{2,1,0:T(4,128)S(1)} %all-gather.4), channel_id=4, replica_groups=mesh['span_0'=4,'span_1'=2,'chord_0'=8,'chord_1'=4] {'chord_1'}, dimensions={0}, use_global_device_ids=true | all-gather | bytes 20480 | tf_op jit(solution)/shard_map/all_gather | solution.py:24
  47.1 12.9 %all-gather.3 = s32[8,8,4,32]{3,1,2,0:T(8,128)S(1)} all-gather(s32[4,8,4,32]{3,1,2,0:T(8,128)S(1)} %copy.78), channel_id=5, replica_groups=mesh['span_0'=4,'span_1'=2,'chord_0'=8,'chord_1'=4] {'span_1'}, dimensions={0}, use_global_device_ids=true | all-gather | bytes 49152 | tf_op jit(solution)/shard_map/all_gather | solution.py:24
  61.6 27.7 %gather_fusion = f32[8192,30]{1,0:T(8,128)} fusion(f32[30,1024]{0,1:T(8,128)S(1)} %copy.81, s32[8192]{0:T(1024)S(1)} %broadcast_clamp_fusion), kind=kCustom, calls=%fused_computation.8 | custom fusion | bytes 1998848 | tf_op jit(solution)/shard_map/jit(_take)/gather | solution.py:168
  89.3 10.0 %fusion.25 = f32[32,30]{0,1:T(8,128)S(1)} fusion(f32[32,8192]{1,0:T(8,128)S(1)} %copy-done, f32[8192,30]{1,0:T(8,128)} %gather_fusion, pred[8192]{0:T(1024)(128)(4,1)S(1)} %compare_and_fusion), kind=kOutput, calls=%fused_computation.40 | convolution fusion | flops 94617600 | bytes 2043648 | tf_op jit(solution)/shard_map/dot_general | solution.py:169
  100.4 111.3 %all-gather.7.cloned.1.call-done = f32[8192,33]{1,0:T(8,128)} async-done(((f32[32,33]{1,0:T(8,128)}), f32[8192,33]{1,0:T(8,128)}) %all-gather.7.cloned.1.call-update) | async-done | bytes 1081360 | tf_op jit(solution)/shard_map/all_gather | solution.py:39
  211.7 5.3 %slice_bitcast_fusion = f32[3,8192]{0,1:T(8,128)} fusion(f32[8192,33]{1,0:T(8,128)} %all-gather.7.cloned.1.call-done), kind=kLoop, calls=%fused_computation.33 | loop fusion | bytes 196608 | tf_op jit(solution)/shard_map/transpose | solution.py:43
  217.1 2.8 copy.84
  219.9 4.5 %slice_bitcast_fusion.1 = f32[30,8192]{0,1:T(8,128)} fusion(f32[8192,33]{1,0:T(8,128)} %all-gather.7.cloned.1.call-done), kind=kLoop, calls=%fused_computation.34 | loop fusion | bytes 1966080 | tf_op jit(solution)/shard_map/transpose | solution.py:43
  224.4 2.9 copy.83
  227.2 71.6 %while.14 = (s32[]{:T(128)}, f32[30,2048]{1,0:T(8,128)S(1)}, f32[30,8192]{1,0:T(8,128)S(1)}, f32[3,8192]{1,0:T(4,128)S(1)}, f32[3,2048]{1,0:T(4,128)S(1)}, /*ind...) while((s32[]{:T(128)}, f32[30,2048]{1,0:T(8,128)S(1)}, ...), condition=%wide.region_1.2_spmd.clone, body=%wide.region_0.1_spmd.clone.sunk | while | flops 194109440 | bytes 623829 | solution.py:159
  229.6 2.1 convolution_add_fusion.2
  231.8 2.1 convolution_add_fusion.2
  234.1 2.1 convolution_add_fusion.2
  238.5 2.1 convolution_add_fusion.2
  240.8 2.1 convolution_add_fusion.2
  243.0 2.1 convolution_add_fusion.2
  247.5 2.1 convolution_add_fusion.2
  249.7 2.1 convolution_add_fusion.2
  252.0 2.1 convolution_add_fusion.2
  256.5 2.1 convolution_add_fusion.2
  258.7 2.1 convolution_add_fusion.2
  267.6 2.1 convolution_add_fusion.2
  276.6 2.1 convolution_add_fusion.2
  285.5 2.1 convolution_add_fusion.2
  294.5 2.1 convolution_add_fusion.2
  299.3 27.7 %gather_fusion.1 = f32[8192,30]{1,0:T(8,128)} fusion(f32[30,2048]{0,1:T(8,128)S(1)} %copy.85, s32[8192]{0:T(1024)S(1)} %bitcast_clamp_fusion), kind=kCustom, calls=%fused_computation.9 | custom fusion | bytes 1998848 | tf_op jit(solution)/shard_map/jit(_take)/gather | solution.py:93
  327.0 3.2 copy.113
  335.7 2.2 collective-permute-start.1
  338.9 3.4 collective-permute-start
  345.5 3.7 %collective-permute-start.3 = (f32[5,16,32]{1,0,2:T(8,128)S(1)}, f32[5,16,32]{1,0,2:T(8,128)S(1)}, u32[]{:S(2)}, u32[]{:S(2)}) collective-permute-start(f32[5,16,32]{1,0,2:T(8,128)S(1)} %get-tuple-element.172), channel_id=1, source_target_pairs={{0,31},{1,0},{2,1},{3,2},{4,3},{5,4},{6,5},{7,6},{8,7},{9,8},{10,9... | collective-permute-start | bytes 30728 | tf_op jit(solution)/shard_map/ppermute | solution.py:58
  (177 shorter events, 58.3 us)
Async XLA Ops:
  7.2 82.1 %copy-start = (f32[32,8192]{1,0:T(8,128)S(1)}, f32[32,8192]{1,0:T(8,128)}, u32[]{:S(2)}) copy-start(f32[32,8192]{1,0:T(8,128)} %param.21) | copy-start | bytes 3145732
  7.2 204.5 %all-gather.7.cloned.1.call-start = ((), (), s32[]{:S(2)}) async-start(), calls=%async_computation | async-start | bytes 4210688 | tf_op jit(solution)/shard_map/all_gather | solution.py:39
  89.3 10.0 %copy-start.4 = (f32[3,32]{1,0:T(4,128)S(1)}, f32[3,32]{1,0:T(4,128)}, u32[]{:S(2)}) copy-start(f32[3,32]{1,0:T(4,128)} %param.17) | copy-start | bytes 1156
  89.3 10.8 %copy-start.1 = (f32[3,2048]{1,0:T(4,128)S(1)}, f32[3,2048]{1,0:T(4,128)}, u32[]{:S(2)}) copy-start(f32[3,2048]{1,0:T(4,128)} %param.16) | copy-start | bytes 73732
  89.3 10.9 %copy-start.5 = (s32[1,1,4,32]{3,2,1,0:T(4,128)S(1)}, s32[1,1,4,32]{3,2,1,0:T(4,128)}, u32[]{:S(2)}) copy-start(s32[1,1,4,32]{3,2,1,0:T(4,128)} %param.23) | copy-start | bytes 1540
  89.3 11.0 %copy-start.6 = (s32[1,1,4,32]{3,2,1,0:T(4,128)S(1)}, s32[1,1,4,32]{3,2,1,0:T(4,128)}, u32[]{:S(2)}) copy-start(s32[1,1,4,32]{3,2,1,0:T(4,128)} %param.24) | copy-start | bytes 1540
  89.3 11.0 %copy-start.2 = (s32[64,128]{1,0:T(8,128)S(1)}, s32[64,128]{1,0:T(8,128)}, u32[]{:S(2)}) copy-start(s32[64,128]{1,0:T(8,128)} %param.22) | copy-start | bytes 98308
  330.2 0.8 copy-start.3
  335.7 13.6 %collective-permute-start.1 = (f32[5,16,32]{1,0,2:T(8,128)S(1)}, f32[5,16,32]{1,0,2:T(8,128)S(1)}, u32[]{:S(2)}, u32[]{:S(2)}) collective-permute-start(f32[5,16,32]{1,0,2:T(8,128)S(1)} %get-tuple-element.168), channel_id=1, source_target_pairs={{32,0},{64,32},{96,64},{128,96},{160,128},{192,160},{224,192},{33,... | collective-permute-start | bytes 30728 | tf_op jit(solution)/shard_map/ppermute | solution.py:52
  338.9 11.0 %collective-permute-start = (f32[5,16,32]{1,0,2:T(8,128)S(1)}, f32[5,16,32]{1,0,2:T(8,128)S(1)}, u32[]{:S(2)}, u32[]{:S(2)}) collective-permute-start(f32[5,16,32]{1,0,2:T(8,128)S(1)} %get-tuple-element.170), channel_id=1, source_target_pairs={{0,32},{32,64},{64,96},{96,128},{128,160},{160,192},{192,224},{1,3... | collective-permute-start | bytes 30728 | tf_op jit(solution)/shard_map/ppermute | solution.py:52
  343.3 8.1 %collective-permute-start.2 = (f32[5,16,32]{1,0,2:T(8,128)S(1)}, f32[5,16,32]{1,0,2:T(8,128)S(1)}, u32[]{:S(2)}, u32[]{:S(2)}) collective-permute-start(f32[5,16,32]{1,0,2:T(8,128)S(1)} %get-tuple-element.174), channel_id=1, source_target_pairs={{0,1},{1,2},{2,3},{3,4},{4,5},{5,6},{6,7},{7,8},{8,9},{9,10},{10,1... | collective-permute-start | bytes 30728 | tf_op jit(solution)/shard_map/ppermute | solution.py:58
  345.5 6.9 %collective-permute-start.3 = (f32[5,16,32]{1,0,2:T(8,128)S(1)}, f32[5,16,32]{1,0,2:T(8,128)S(1)}, u32[]{:S(2)}, u32[]{:S(2)}) collective-permute-start(f32[5,16,32]{1,0,2:T(8,128)S(1)} %get-tuple-element.172), channel_id=1, source_target_pairs={{0,31},{1,0},{2,1},{3,2},{4,3},{5,4},{6,5},{7,6},{8,7},{9,8},{10,9... | collective-permute-start | bytes 30728 | tf_op jit(solution)/shard_map/ppermute | solution.py:58
Sparse Core Ops, SparseCore 0:
  100.2 111.5 all-gather.6
where the time goes:
time: 361 us
  waiting for transfers between devices  112 us (31%)
  local copies, waits for them, and re-layouts  88.7 us (25%)
  matrix products  78.6 us (22%)
  blocking collectives  49.8 us (14%)
  between operations  15.3 us (4%)
  starting transfers between devices  10.5 us (3%)
  other arithmetic  4.66 us (1%)
    all_gather x1, waiting for transfers between devices, gather_turned(): whole = lax.all_gather(both, axis, axis=0, tiled=True)  111 us
    dot_general x32, matrix products, step(): jnp.dot(weight_block, kernel, precision=lax.Precision.HIGHEST, preferred_...  67.3 us
    all_gather x3, blocking collectives, stacked_from(): parts = lax.all_gather(parts, axes[k])  42 us
    gather x2, local copies, waits for them, and re-layouts, element_metrics(): jnp.take(jnp.concatenate([moved, node_rows[3 * sections:]], axis=0), link...  30.9 us
    gather x1, local copies, waits for them, and re-layouts, on_device(): right_side = jnp.take(table, every_id, axis=1)  27.7 us
    dot_general x1, matrix products, on_device(): lax.dot_general(right_side, minv, (((1,), (1,)), ((), ())), precision=hig...  9.97 us
    transpose x2, local copies, waits for them, and re-layouts, gather_turned(): jnp.moveaxis(b.reshape(-1, *t.shape[1:]), 0, dim)  9.81 us
    unnamed x20, local copies, waits for them, and re-layouts  8.74 us
  transfers between devices with their start and end apart: 5, of which 2 were waited for; matrix products, arithmetic and copies ran while one was open for 2% of the time, Pallas kernels for 0%

commit v1 on v0

--- a/solution.py
+++ b/solution.py
@@ -36,7 +36,9 @@
     turned = [jnp.moveaxis(a, dim, 0) for a, dim in zip(arrays, dims)]
     widths = [t[0].size for t in turned]
     both = jnp.concatenate([t.reshape(-1, w) for t, w in zip(turned, widths)], axis=1)
-    whole = lax.all_gather(both, axis, axis=0, tiled=True)
+    whole = jnp.concatenate(
+        lax.all_to_all(jnp.stack([both] * lax.axis_size(axis)), axis, 0, 0), axis=0
+    )
     parts = jnp.split(whole, [sum(widths[:k]) for k in range(1, len(widths))], axis=1)
     return tuple(
         (

time: 361 us -> 292 us (0.81)
  waiting for transfers between devices: 112 us -> 32.9 us
  between operations: 15.3 us -> 1.9 us
  local copies, waits for them, and re-layouts: 88.7 us -> 101 us
  starting transfers between devices: 10.5 us -> 18 us
    all_gather x1 -> x0, waiting for transfers between devices: 111 us -> none  [gather_turned(): whole = lax.all_gather(both, axis, axis=0, tiled=True)]
    all_to_all x0 -> x1, waiting for transfers between devices: none -> 32.9 us  [gather_turned(): lax.all_to_all(jnp.stack([both] * lax.axis_size(axis)), axis, 0, 0)]
    unnamed x20 -> x26, local copies, waits for them, and re-layouts: 8.74 us -> 22.9 us
    transpose x2 -> x0, local copies, waits for them, and re-layouts: 9.81 us -> none  [gather_turned(): jnp.moveaxis(b.reshape(-1, *t.shape[1:]), 0, dim)]
    all_to_all x0 -> x1, starting transfers between devices: none -> 7.24 us  [gather_turned(): lax.all_to_all(jnp.stack([both] * lax.axis_size(axis)), axis, 0, 0)]
    split x0 -> x1, local copies, waits for them, and re-layouts: none -> 5.33 us  [gather_turned(): jnp.split(whole, [sum(widths[:k]) for k in range(1, len(widths))], axis=1)]
  transfers between devices with their start and end apart: 5 -> 5, of which waited for: 2 -> 1; matrix products, arithmetic and copies ran while one was open for 2% -> 2% of each run, Pallas kernels for 0% -> 0%
where the time goes in v1:
time: 292 us
  local copies, waits for them, and re-layouts  101 us (35%)
  matrix products  78.6 us (27%)
  blocking collectives  49.8 us (17%)
  waiting for transfers between devices  32.9 us (11%)
  starting transfers between devices  18 us (6%)
  other arithmetic  8.1 us (3%)
    dot_general x32, matrix products, step(): jnp.dot(weight_block, kernel, precision=lax.Precision.HIGHEST, preferred_...  67.3 us
    all_gather x3, blocking collectives, stacked_from(): parts = lax.all_gather(parts, axes[k])  42 us
    all_to_all x1, waiting for transfers between devices, gather_turned(): lax.all_to_all(jnp.stack([both] * lax.axis_size(axis)), axis, 0, 0)  32.9 us
    gather x2, local copies, waits for them, and re-layouts, element_metrics(): jnp.take(jnp.concatenate([moved, node_rows[3 * sections:]], axis=0), link...  30.8 us
    gather x1, local copies, waits for them, and re-layouts, on_device(): right_side = jnp.take(table, every_id, axis=1)  27.8 us
    unnamed x26, local copies, waits for them, and re-layouts  22.9 us
    dot_general x1, matrix products, on_device(): lax.dot_general(right_side, minv, (((1,), (1,)), ((), ())), precision=hig...  9.95 us
    unnamed x1, blocking collectives  7.85 us
  transfers between devices with their start and end apart: 5, of which 1 were waited for; matrix products, arithmetic and copies ran while one was open for 2% of the time, Pallas kernels for 0%

profile of v1, /device:TPU:1, one launch (start us, length us, event | category | flops | bytes accessed | tf_op | source)
XLA Modules:
  0.0 291.9 jit_solution(9548399872651170710)
XLA Ops:
  3.5 7.8 %all-reduce = s32[128]{0:T(128)S(1)} all-reduce(s32[128]{0:T(128)S(1)} %dynamic-update-slice), channel_id=2, replica_groups=mesh['span_0'=4,'span_1'=2,'chord_0'=8,'chord_1'=4] {'span_0'}, use_global_device_ids=true, to_apply=%add | all-reduce | flops 128 | bytes 1024
  11.5 19.8 %all-gather.4 = s32[8,4,32]{2,1,0:T(4,128)S(1)} all-gather(s32[1,4,32]{2,1,0:T(4,128)S(1)} %reshape.728), channel_id=3, replica_groups=mesh['span_0'=4,'span_1'=2,'chord_0'=8,'chord_1'=4] {'chord_0'}, dimensions={0}, use_global_device_ids=true | all-gather | bytes 4608 | tf_op jit(solution)/shard_map/all_gather | solution.py:24
  31.2 9.3 %all-gather.2 = s32[32,4,32]{2,1,0:T(4,128)S(1)} all-gather(s32[8,4,32]{2,1,0:T(4,128)S(1)} %all-gather.4), channel_id=4, replica_groups=mesh['span_0'=4,'span_1'=2,'chord_0'=8,'chord_1'=4] {'chord_1'}, dimensions={0}, use_global_device_ids=true | all-gather | bytes 20480 | tf_op jit(solution)/shard_map/all_gather | solution.py:24
  40.6 12.9 %all-gather.3 = s32[8,8,4,32]{3,1,2,0:T(8,128)S(1)} all-gather(s32[4,8,4,32]{3,1,2,0:T(8,128)S(1)} %copy.78), channel_id=5, replica_groups=mesh['span_0'=4,'span_1'=2,'chord_0'=8,'chord_1'=4] {'span_1'}, dimensions={0}, use_global_device_ids=true | all-gather | bytes 49152 | tf_op jit(solution)/shard_map/all_gather | solution.py:24
  55.0 27.8 %gather_fusion = f32[8192,30]{1,0:T(8,128)} fusion(f32[30,1024]{0,1:T(8,128)S(1)} %copy.81, s32[8192]{0:T(1024)S(1)} %broadcast_clamp_fusion), kind=kCustom, calls=%fused_computation.8 | custom fusion | bytes 1998848 | tf_op jit(solution)/shard_map/jit(_take)/gather | solution.py:170
  82.8 9.9 %fusion.25 = f32[32,30]{0,1:T(8,128)S(1)} fusion(f32[32,8192]{1,0:T(8,128)S(1)} %copy-done, f32[8192,30]{1,0:T(8,128)} %gather_fusion, pred[8192]{0:T(1024)(128)(4,1)S(1)} %compare_and_fusion), kind=kOutput, calls=%fused_computation.38 | convolution fusion | flops 94617600 | bytes 2043648 | tf_op jit(solution)/shard_map/dot_general | solution.py:171
  92.8 2.5 stack.28
  95.3 7.3 %reshape.751 = f32[256,1,1056]{2,1,0:T(1,128)} reshape(f32[256,32,33]{2,1,0:T(8,128)} %stack.28) | data formatting | bytes 2162688
  102.7 7.2 %all-to-all-start = ((f32[256,1,1056]{2,1,0:T(1,128)}), f32[256,1,1056]{2,1,0:T(1,128)S(1)}, u32[]{:S(2)}, u32[]{:S(2)}) async-start(f32[256,1,1056]{2,1,0:T(1,128)} %reshape.751), calls=%async_computation | async-start | bytes 2359296 | tf_op jit(solution)/shard_map/all_to_all | solution.py:40
  110.9 32.9 %all-to-all-done = f32[256,1,1056]{2,1,0:T(1,128)S(1)} async-done(((f32[256,1,1056]{2,1,0:T(1,128)}), f32[256,1,1056]{2,1,0:T(1,128)S(1)}, u32[]{:S(2)}, u32[]{:S(2)}) %all-to-all-start) | async-done | bytes 1081376 | tf_op jit(solution)/shard_map/all_to_all | solution.py:40
  144.3 3.4 %reduce = f32[256,1056]{1,0:T(8,128)S(1)} reduce(f32[256,1,1056]{2,1,0:T(1,128)S(1)} %all-to-all-done, f32[]{:T(128)} %broadcast.222), dimensions={1}, to_apply=%all_to_all.3.reduce_sub_computation | reduce | bytes 2162692 | tf_op jit(solution)/shard_map/all_to_all | solution.py:40
  147.8 6.8 %reshape.752 = f32[256,32,33]{2,1,0:T(8,128)} reshape(f32[256,1056]{1,0:T(8,128)S(1)} %reduce) | data formatting | bytes 2162688
  154.5 5.3 %split.9 = f32[8192,3]{1,0:T(8,128)} slice(f32[8192,33]{1,0:T(8,128)} %bitcast.183), slice={[0:8192], [30:33]} | slice | bytes 196608 | tf_op jit(solution)/shard_map/split | solution.py:42
  159.8 2.8 copy.115
  162.7 2.9 copy.114
  165.6 71.7 %while.14 = (s32[]{:T(128)}, f32[30,2048]{1,0:T(8,128)S(1)}, f32[30,8192]{1,0:T(8,128)S(1)}, f32[3,8192]{1,0:T(4,128)S(1)}, f32[3,2048]{1,0:T(4,128)S(1)}, /*ind...) while((s32[]{:T(128)}, f32[30,2048]{1,0:T(8,128)S(1)}, ...), condition=%wide.region_1.2_spmd.clone, body=%wide.region_0.1_spmd.clone.sunk | while | flops 194109440 | bytes 623821 | solution.py:161
  168.0 2.1 convolution_add_fusion.2
  170.2 2.1 convolution_add_fusion.2
  172.5 2.1 convolution_add_fusion.2
  174.7 2.1 convolution_add_fusion.2
  177.0 2.1 convolution_add_fusion.2
  179.2 2.1 convolution_add_fusion.2
  181.4 2.1 convolution_add_fusion.2
  183.7 2.1 convolution_add_fusion.2
  185.9 2.1 convolution_add_fusion.2
  188.2 2.1 convolution_add_fusion.2
  190.4 2.1 convolution_add_fusion.2
  192.6 2.1 convolution_add_fusion.2
  237.8 27.8 %gather_fusion.1 = f32[8192,30]{1,0:T(8,128)} fusion(f32[30,2048]{0,1:T(8,128)S(1)} %copy.84, s32[8192]{0:T(1024)S(1)} %bitcast_clamp_fusion), kind=kCustom, calls=%fused_computation.9 | custom fusion | bytes 1998848 | tf_op jit(solution)/shard_map/jit(_take)/gather | solution.py:95
  265.5 3.1 %copy.113 = f32[64,128,30]{1,0,2:T(8,128)S(1)} copy(f32[64,128,30]{2,1,0:T(8,128)} %bitcast.188) | data formatting | bytes 1966080 | tf_op jit(solution)/shard_map/jit(_take)/gather | solution.py:95
  276.2 3.7 %collective-permute-start = (f32[5,16,32]{1,0,2:T(8,128)S(1)}, f32[5,16,32]{1,0,2:T(8,128)S(1)}, u32[]{:S(2)}, u32[]{:S(2)}) collective-permute-start(f32[5,16,32]{1,0,2:T(8,128)S(1)} %get-tuple-element.165), channel_id=1, source_target_pairs={{0,32},{32,64},{64,96},{96,128},{128,160},{160,192},{192,224},{1,3... | collective-permute-start | bytes 30728 | tf_op jit(solution)/shard_map/ppermute | solution.py:54
  282.6 4.1 %collective-permute-start.3 = (f32[5,16,32]{1,0,2:T(8,128)S(1)}, f32[5,16,32]{1,0,2:T(8,128)S(1)}, u32[]{:S(2)}, u32[]{:S(2)}) collective-permute-start(f32[5,16,32]{1,0,2:T(8,128)S(1)} %get-tuple-element.167), channel_id=1, source_target_pairs={{0,31},{1,0},{2,1},{3,2},{4,3},{5,4},{6,5},{7,6},{8,7},{9,8},{10,9... | collective-permute-start | bytes 30728 | tf_op jit(solution)/shard_map/ppermute | solution.py:60
  (184 shorter events, 66.1 us)
Async XLA Ops:
  0.6 82.2 %copy-start = (f32[32,8192]{1,0:T(8,128)S(1)}, f32[32,8192]{1,0:T(8,128)}, u32[]{:S(2)}) copy-start(f32[32,8192]{1,0:T(8,128)} %param.21) | copy-start | bytes 3145732
  82.8 10.0 %copy-start.6 = (f32[3,32]{1,0:T(4,128)S(1)}, f32[3,32]{1,0:T(4,128)}, u32[]{:S(2)}) copy-start(f32[3,32]{1,0:T(4,128)} %param.17) | copy-start | bytes 1156
  102.6 7.3 %copy-start.1 = (f32[3,2048]{1,0:T(4,128)S(1)}, f32[3,2048]{1,0:T(4,128)}, u32[]{:S(2)}) copy-start(f32[3,2048]{1,0:T(4,128)} %param.16) | copy-start | bytes 73732
  102.6 8.0 %copy-start.7 = (s32[1,1,4,32]{3,2,1,0:T(4,128)S(1)}, s32[1,1,4,32]{3,2,1,0:T(4,128)}, u32[]{:S(2)}) copy-start(s32[1,1,4,32]{3,2,1,0:T(4,128)} %param.23) | copy-start | bytes 1540
  102.6 8.1 %copy-start.8 = (s32[1,1,4,32]{3,2,1,0:T(4,128)S(1)}, s32[1,1,4,32]{3,2,1,0:T(4,128)}, u32[]{:S(2)}) copy-start(s32[1,1,4,32]{3,2,1,0:T(4,128)} %param.24) | copy-start | bytes 1540
  102.6 8.2 %copy-start.4 = (s32[64,128]{1,0:T(8,128)S(1)}, s32[64,128]{1,0:T(8,128)}, u32[]{:S(2)}) copy-start(s32[64,128]{1,0:T(8,128)} %param.22) | copy-start | bytes 98308
  102.7 41.1 %all-to-all-start = ((f32[256,1,1056]{2,1,0:T(1,128)}), f32[256,1,1056]{2,1,0:T(1,128)S(1)}, u32[]{:S(2)}, u32[]{:S(2)}) async-start(f32[256,1,1056]{2,1,0:T(1,128)} %reshape.751), calls=%async_computation | async-start | bytes 2359296 | tf_op jit(solution)/shard_map/all_to_all | solution.py:40
  162.7 2.9 %copy-start.3 = (f32[30,2048]{1,0:T(8,128)S(1)}, f32[30,2048]{1,0:T(8,128)}, u32[]{:S(2)}) copy-start(f32[30,2048]{1,0:T(8,128)} %custom-call) | copy-start | bytes 737284
  165.6 71.7 %copy-start.2 = (f32[15,2048]{1,0:T(8,128)S(1)}, f32[15,2048]{1,0:T(8,128)}, u32[]{:S(2)}) copy-start(f32[15,2048]{1,0:T(8,128)} %tile.10) | copy-start | bytes 368644
  268.6 0.8 copy-start.5
  273.1 14.8 %collective-permute-start.1 = (f32[5,16,32]{1,0,2:T(8,128)S(1)}, f32[5,16,32]{1,0,2:T(8,128)S(1)}, u32[]{:S(2)}, u32[]{:S(2)}) collective-permute-start(f32[5,16,32]{1,0,2:T(8,128)S(1)} %get-tuple-element.163), channel_id=1, source_target_pairs={{32,0},{64,32},{96,64},{128,96},{160,128},{192,160},{224,192},{33,... | collective-permute-start | bytes 30728 | tf_op jit(solution)/shard_map/ppermute | solution.py:54
  276.2 12.4 %collective-permute-start = (f32[5,16,32]{1,0,2:T(8,128)S(1)}, f32[5,16,32]{1,0,2:T(8,128)S(1)}, u32[]{:S(2)}, u32[]{:S(2)}) collective-permute-start(f32[5,16,32]{1,0,2:T(8,128)S(1)} %get-tuple-element.165), channel_id=1, source_target_pairs={{0,32},{32,64},{64,96},{96,128},{128,160},{160,192},{192,224},{1,3... | collective-permute-start | bytes 30728 | tf_op jit(solution)/shard_map/ppermute | solution.py:54
  280.8 8.5 %collective-permute-start.2 = (f32[5,16,32]{1,0,2:T(8,128)S(1)}, f32[5,16,32]{1,0,2:T(8,128)S(1)}, u32[]{:S(2)}, u32[]{:S(2)}) collective-permute-start(f32[5,16,32]{1,0,2:T(8,128)S(1)} %get-tuple-element.169), channel_id=1, source_target_pairs={{0,1},{1,2},{2,3},{3,4},{4,5},{5,6},{6,7},{7,8},{8,9},{9,10},{10,1... | collective-permute-start | bytes 30728 | tf_op jit(solution)/shard_map/ppermute | solution.py:60
  282.6 7.7 %collective-permute-start.3 = (f32[5,16,32]{1,0,2:T(8,128)S(1)}, f32[5,16,32]{1,0,2:T(8,128)S(1)}, u32[]{:S(2)}, u32[]{:S(2)}) collective-permute-start(f32[5,16,32]{1,0,2:T(8,128)S(1)} %get-tuple-element.167), channel_id=1, source_target_pairs={{0,31},{1,0},{2,1},{3,2},{4,3},{5,4},{6,5},{7,6},{8,7},{9,8},{10,9... | collective-permute-start | bytes 30728 | tf_op jit(solution)/shard_map/ppermute | solution.py:60
